TPU v7x, 32 devices: a whole 2x2x4 slice. The times are simulated.
32 devices in a mesh: ctx: 8 (over y, x, core), fsdp: 4 (over z).
Axes of the slice: x: 2, y: 2, z: 4, core: 2. Of those that a mesh axis runs over, the one named last changes fastest.
Arguments:
- tokens: bfloat16 [4096, 1600], P(('fsdp', 'ctx')), may hold values from -6 to 6
- block_table: int32 [8, 2], replicated, may hold values from 0 to 15, as said below
- ln1_gain: bfloat16 [1600], P('fsdp'), may hold values from 0.099609375 to 1.8984375
- ln1_bias: bfloat16 [1600], P('fsdp'), may hold values from -1.75 to 1.75
- qkv_weight: bfloat16 [1600, 4800], P('fsdp'), may hold values from -0.15625 to 0.15625
- query_bias: bfloat16 [1600], P('fsdp'), may hold values from -3 to 3
- value_bias: bfloat16 [1600], P('fsdp'), may hold values from -0.875 to 0.875
- proj_weight: bfloat16 [1600, 1600], P('fsdp'), may hold values from -1.25 to 1.25
- proj_bias: bfloat16 [1600], P('fsdp'), may hold values from -1.75 to 1.75
- ln2_gain: bfloat16 [1600], P('fsdp'), may hold values from 0.099609375 to 1.8984375
- ln2_bias: bfloat16 [1600], P('fsdp'), may hold values from -1.75 to 1.75
- fc_weight: bfloat16 [1600, 6400], P('fsdp'), may hold values from -0.15625 to 0.15625
- fc_bias: bfloat16 [6400], P('fsdp'), may hold values from -3 to 3
- out_weight: bfloat16 [6400, 1600], P('fsdp'), may hold values from -0.078125 to 0.078125
- out_bias: bfloat16 [1600], P('fsdp'), may hold values from -1.75 to 1.75
- cotangent: bfloat16 [4096, 1600], P(('fsdp', 'ctx')), may hold values from -6 to 6
Outputs:
- layer_out: bfloat16 [4096, 1600], P(('fsdp', 'ctx'))
- grad_tokens: bfloat16 [4096, 1600], P(('fsdp', 'ctx'))
- grad_ln1_gain: float32 [1600], P('fsdp')
- grad_ln1_bias: float32 [1600], P('fsdp')
- grad_qkv_weight: float32 [1600, 4800], P('fsdp')
- grad_query_bias: float32 [1600], P('fsdp')
- grad_value_bias: float32 [1600], P('fsdp')
- grad_proj_weight: float32 [1600, 1600], P('fsdp')
- grad_proj_bias: float32 [1600], P('fsdp')
- grad_ln2_gain: float32 [1600], P('fsdp')
- grad_ln2_bias: float32 [1600], P('fsdp')
- grad_fc_weight: float32 [1600, 6400], P('fsdp')
- grad_fc_bias: float32 [6400], P('fsdp')
- grad_out_weight: float32 [6400, 1600], P('fsdp')
- grad_out_bias: float32 [1600], P('fsdp')
Inputs may be any that keep to these rules, and one draw needn't show every extreme that they name: `block_table`: row i is (p_i, 15 - p_i) with p_i below 8; every block number appears exactly once.
All inputs are finite; a program needn't handle non-finite values.
Results may differ from a plain program's by a relative error of at most 0.02.
Values may be sent and summed in bfloat16 or wider, within the bound.
A program may use at most 256 MiB of HBM per device.

v0:
```python
import math
import jax
import jax.numpy as jnp
from jax import lax
from jax.sharding import PartitionSpec as P

HEADS = 25


def layer_norm(values, gain_vec, shift_vec):
    centre = values - jnp.mean(values, axis=-1, keepdims=True)
    spread = jnp.mean(centre * centre, axis=-1, keepdims=True)
    return centre * lax.rsqrt(spread + 1e-05) * gain_vec + shift_vec


def gelu_tanh(values):
    return jax.nn.gelu(values, approximate=True)


def body(
    tokens,
    block_table,
    ln1_gain,
    ln1_bias,
    qkv_weight,
    query_bias,
    value_bias,
    proj_weight,
    proj_bias,
    ln2_gain,
    ln2_bias,
    fc_weight,
    fc_bias,
    out_weight,
    out_bias,
    cotangent,
):
    row_count = tokens.shape[0]
    model_width = tokens.shape[1]
    block_rows = row_count // 2
    head_dim = model_width // HEADS
    score_scale = head_dim ** (-0.5)
    ctx_index = lax.axis_index("ctx")
    own_blocks = lax.dynamic_slice_in_dim(block_table, ctx_index, 1, 0).reshape(-1)
    offsets = jnp.arange(block_rows, dtype=jnp.int32)
    query_pos = (own_blocks[:, None] * block_rows + offsets[None, :]).reshape(-1)
    key_pos = (block_table.reshape(-1)[:, None] * block_rows + offsets[None, :]).reshape(-1)
    seq_len = key_pos.shape[0]
    key_block = math.gcd(seq_len, 512)
    block_count = seq_len // key_block
    pos_blocks = key_pos.reshape(block_count, key_block)
    gain_one, shift_one, qkv_full, q_bias, v_bias, proj_full, proj_b = (
        lax.all_gather(ln1_gain, "fsdp", axis=0, tiled=True),
        lax.all_gather(ln1_bias, "fsdp", axis=0, tiled=True),
        lax.all_gather(qkv_weight, "fsdp", axis=0, tiled=True),
        lax.all_gather(query_bias, "fsdp", axis=0, tiled=True),
        lax.all_gather(value_bias, "fsdp", axis=0, tiled=True),
        lax.all_gather(proj_weight, "fsdp", axis=0, tiled=True),
        lax.all_gather(proj_bias, "fsdp", axis=0, tiled=True),
    )
    inputs = tokens.astype(jnp.float32)
    gain_one_f = gain_one.astype(jnp.float32)
    shift_one_f = shift_one.astype(jnp.float32)
    normed_one = layer_norm(inputs, gain_one_f, shift_one_f).astype(jnp.bfloat16)
    bias_row = jnp.concatenate([q_bias, jnp.zeros_like(q_bias), v_bias]).astype(jnp.float32)
    joined = jnp.dot(normed_one, qkv_full, preferred_element_type=jnp.float32) + bias_row
    query_rows = joined[:, :model_width].astype(jnp.bfloat16).reshape(row_count, HEADS, head_dim)
    key_local = joined[:, model_width : 2 * model_width].astype(jnp.bfloat16)
    value_local = joined[:, 2 * model_width :].astype(jnp.bfloat16)
    key_all, value_all = (
        lax.all_gather(key_local, "ctx", axis=0, tiled=True),
        lax.all_gather(value_local, "ctx", axis=0, tiled=True),
    )

    def scores_of(key_tile, pos_tile):
        raw_scores = jnp.einsum(
            "qhd,khd->hqk", query_rows, key_tile, preferred_element_type=jnp.float32
        )
        allowed = pos_tile[None, :] <= query_pos[:, None]
        return (jnp.where(allowed[None], raw_scores * score_scale, -1e30), allowed)

    key_tiles = key_all.reshape(block_count, key_block, HEADS, head_dim)
    value_tiles = value_all.reshape(block_count, key_block, HEADS, head_dim)

    def stat_step(carried, tile_set):
        top_prev, total_prev = carried
        scores, allowed = scores_of(tile_set[0], tile_set[1])
        top_new = jnp.maximum(top_prev, jnp.max(scores, axis=-1))
        total_new = total_prev * jnp.exp(top_prev - top_new) + jnp.sum(
            jnp.exp(scores - top_new[..., None]), axis=-1
        )
        return ((top_new, total_new), None)

    start_stats = (
        jnp.full((HEADS, row_count), -1e30, jnp.float32),
        jnp.zeros((HEADS, row_count), jnp.float32),
    )
    (top_all, total_all), _ = lax.scan(stat_step, start_stats, (key_tiles, pos_blocks))
    log_total = top_all + jnp.log(total_all)

    def out_step(summed, tile_set):
        scores, allowed = scores_of(tile_set[0], tile_set[2])
        soft_w = jnp.exp(scores - log_total[..., None]).astype(jnp.bfloat16)
        return (
            summed
            + jnp.einsum("hqk,khd->qhd", soft_w, tile_set[1], preferred_element_type=jnp.float32),
            None,
        )

    heads_f, _ = lax.scan(
        out_step,
        jnp.zeros((row_count, HEADS, head_dim), jnp.float32),
        (key_tiles, value_tiles, pos_blocks),
    )
    heads_low = heads_f.reshape(row_count, model_width).astype(jnp.bfloat16)
    middle = (
        inputs
        + jnp.dot(heads_low, proj_full, preferred_element_type=jnp.float32)
        + proj_b.astype(jnp.float32)
    )
    fsdp_count = lax.axis_size("fsdp")
    width_share = model_width // fsdp_count
    small_stack = jnp.stack([ln2_gain, ln2_bias, out_bias], axis=1)
    small_tiled = jnp.tile(small_stack, (1, fsdp_count))
    fc_cols, small_full = (
        lax.all_to_all(fc_weight, "fsdp", split_axis=1, concat_axis=0, tiled=True),
        lax.all_to_all(small_tiled, "fsdp", split_axis=1, concat_axis=0, tiled=True),
    )
    gain_two_f = small_full[:, 0].astype(jnp.float32)
    shift_two_f = small_full[:, 1].astype(jnp.float32)
    out_b_f = small_full[:, 2].astype(jnp.float32)
    normed_two = layer_norm(middle, gain_two_f, shift_two_f).astype(jnp.bfloat16)
    group_normed, group_upstream = (
        lax.all_gather(normed_two, "fsdp", axis=0, tiled=True),
        lax.all_gather(cotangent, "fsdp", axis=0, tiled=True),
    )
    hidden_pre = jnp.dot(
        group_normed, fc_cols, preferred_element_type=jnp.float32
    ) + fc_bias.astype(jnp.float32)
    hidden = gelu_tanh(hidden_pre).astype(jnp.bfloat16)
    rows = hidden
    summed_out = lax.psum_scatter(
        jnp.dot(rows, out_weight, preferred_element_type=jnp.float32).astype(jnp.bfloat16),
        "fsdp",
        scatter_dimension=0,
        tiled=True,
    ).astype(jnp.float32)
    output = middle + summed_out + out_b_f
    out_rows = output.astype(jnp.bfloat16)
    owned_ow = jnp.einsum("tf,td->fd", hidden, group_upstream, preferred_element_type=jnp.float32)
    full_out_b = jnp.sum(group_upstream.astype(jnp.float32), axis=0)
    owned_ob = lax.dynamic_slice_in_dim(
        full_out_b, lax.axis_index("fsdp") * width_share, width_share, 0
    )
    grad_hidden = jnp.einsum(
        "td,fd->tf", group_upstream, out_weight, preferred_element_type=jnp.float32
    )
    _, gelu_pull = jax.vjp(gelu_tanh, hidden_pre)
    grad_pre = gelu_pull(grad_hidden)[0].astype(jnp.bfloat16)
    grad_fc_cols = jnp.einsum(
        "tc,tf->cf", group_normed, grad_pre, preferred_element_type=jnp.float32
    )
    owned_fcb = jnp.sum(grad_pre.astype(jnp.float32), axis=0)
    rows = grad_pre
    grad_normed_two = lax.psum_scatter(
        jnp.einsum("tf,cf->tc", rows, fc_cols, preferred_element_type=jnp.float32).astype(
            jnp.bfloat16
        ),
        "fsdp",
        scatter_dimension=0,
        tiled=True,
    ).astype(jnp.float32)
    _, norm_pull_two = jax.vjp(layer_norm, middle, gain_two_f, shift_two_f)
    grad_mid_norm, grad_gain_two, grad_shift_two = norm_pull_two(grad_normed_two)
    grad_middle = cotangent.astype(jnp.float32) + grad_mid_norm
    norm_pair = jnp.stack([grad_gain_two, grad_shift_two], axis=1)
    owned_fcw, norm_parts = (
        lax.all_to_all(
            grad_fc_cols.astype(jnp.bfloat16), "fsdp", split_axis=0, concat_axis=1, tiled=True
        ).astype(grad_fc_cols.dtype),
        lax.all_to_all(
            norm_pair.astype(jnp.bfloat16), "fsdp", split_axis=0, concat_axis=1, tiled=True
        ).astype(norm_pair.dtype),
    )
    norm_sums = jnp.sum(norm_parts.reshape(width_share, fsdp_count, 2), axis=1)
    owned_g2 = norm_sums[:, 0]
    owned_b2 = norm_sums[:, 1]
    total_g2, total_b2, total_fcw, total_fcb, total_ow, total_ob = (
        lax.psum(owned_g2.astype(jnp.bfloat16), "ctx").astype(jnp.float32),
        lax.psum(owned_b2.astype(jnp.bfloat16), "ctx").astype(jnp.float32),
        lax.psum(owned_fcw.astype(jnp.bfloat16), "ctx").astype(jnp.float32),
        lax.psum(owned_fcb.astype(jnp.bfloat16), "ctx").astype(jnp.float32),
        lax.psum(owned_ow.astype(jnp.bfloat16), "ctx").astype(jnp.float32),
        lax.psum(owned_ob.astype(jnp.bfloat16), "ctx").astype(jnp.float32),
    )
    grad_branch = grad_middle.astype(jnp.bfloat16)
    grad_proj_w = jnp.einsum(
        "tc,td->cd", heads_low, grad_branch, preferred_element_type=jnp.float32
    )
    grad_proj_b = jnp.sum(grad_branch.astype(jnp.float32), axis=0)
    grad_heads = jnp.einsum(
        "td,cd->tc", grad_branch, proj_full, preferred_element_type=jnp.float32
    ).astype(jnp.bfloat16)
    grad_heads_split = grad_heads.reshape(row_count, HEADS, head_dim)
    delta_rows = jnp.sum(grad_heads_split.astype(jnp.float32) * heads_f, axis=-1).T

    def grad_step(grad_query, tile_set):
        key_tile, value_tile, pos_tile = tile_set
        scores, allowed = scores_of(key_tile, pos_tile)
        soft_w = jnp.exp(scores - log_total[..., None])
        grad_soft = jnp.einsum(
            "qhd,khd->hqk", grad_heads_split, value_tile, preferred_element_type=jnp.float32
        )
        grad_raw = jnp.where(
            allowed[None], soft_w * (grad_soft - delta_rows[..., None]) * score_scale, 0.0
        ).astype(jnp.bfloat16)
        grad_query = grad_query + jnp.einsum(
            "hqk,khd->qhd", grad_raw, key_tile, preferred_element_type=jnp.float32
        )
        grad_key = jnp.einsum(
            "hqk,qhd->khd", grad_raw, query_rows, preferred_element_type=jnp.float32
        )
        grad_value = jnp.einsum(
            "hqk,qhd->khd",
            soft_w.astype(jnp.bfloat16),
            grad_heads_split,
            preferred_element_type=jnp.float32,
        )
        return (grad_query, (grad_key, grad_value))

    grad_query, (key_grads, value_grads) = lax.scan(
        grad_step,
        jnp.zeros((row_count, HEADS, head_dim), jnp.float32),
        (key_tiles, value_tiles, pos_blocks),
    )
    key_terms = key_grads.reshape(seq_len, model_width)
    value_terms = value_grads.reshape(seq_len, model_width)
    key_mine, value_mine = (
        lax.psum_scatter(
            key_terms.astype(jnp.bfloat16), "ctx", scatter_dimension=0, tiled=True
        ).astype(jnp.float32),
        lax.psum_scatter(
            value_terms.astype(jnp.bfloat16), "ctx", scatter_dimension=0, tiled=True
        ).astype(jnp.float32),
    )
    grad_joined = jnp.concatenate(
        [grad_query.reshape(row_count, model_width), key_mine, value_mine], axis=1
    ).astype(jnp.bfloat16)
    grad_q_bias = jnp.sum(grad_joined[:, :model_width].astype(jnp.float32), axis=0)
    grad_v_bias = jnp.sum(grad_joined[:, 2 * model_width :].astype(jnp.float32), axis=0)
    grad_qkv_w = jnp.einsum(
        "tc,tk->ck", normed_one, grad_joined, preferred_element_type=jnp.float32
    )
    grad_normed_one = jnp.einsum(
        "tk,ck->tc", grad_joined, qkv_full, preferred_element_type=jnp.float32
    )
    _, norm_pull_one = jax.vjp(layer_norm, inputs, gain_one_f, shift_one_f)
    grad_in_norm, grad_gain_one, grad_shift_one = norm_pull_one(grad_normed_one)
    grad_inputs = (grad_middle + grad_in_norm).astype(jnp.bfloat16)
    owned_g1, owned_b1, owned_qkv, owned_qb, owned_vb, owned_pw, owned_pb = (
        lax.psum_scatter(
            grad_gain_one.astype(jnp.bfloat16), "fsdp", scatter_dimension=0, tiled=True
        ).astype(jnp.float32),
        lax.psum_scatter(
            grad_shift_one.astype(jnp.bfloat16), "fsdp", scatter_dimension=0, tiled=True
        ).astype(jnp.float32),
        lax.psum_scatter(
            grad_qkv_w.astype(jnp.bfloat16), "fsdp", scatter_dimension=0, tiled=True
        ).astype(jnp.float32),
        lax.psum_scatter(
            grad_q_bias.astype(jnp.bfloat16), "fsdp", scatter_dimension=0, tiled=True
        ).astype(jnp.float32),
        lax.psum_scatter(
            grad_v_bias.astype(jnp.bfloat16), "fsdp", scatter_dimension=0, tiled=True
        ).astype(jnp.float32),
        lax.psum_scatter(
            grad_proj_w.astype(jnp.bfloat16), "fsdp", scatter_dimension=0, tiled=True
        ).astype(jnp.float32),
        lax.psum_scatter(
            grad_proj_b.astype(jnp.bfloat16), "fsdp", scatter_dimension=0, tiled=True
        ).astype(jnp.float32),
    )
    total_g1, total_b1, total_qkv, total_qb, total_vb, total_pw, total_pb = (
        lax.psum(owned_g1.astype(jnp.bfloat16), "ctx").astype(jnp.float32),
        lax.psum(owned_b1.astype(jnp.bfloat16), "ctx").astype(jnp.float32),
        lax.psum(owned_qkv.astype(jnp.bfloat16), "ctx").astype(jnp.float32),
        lax.psum(owned_qb.astype(jnp.bfloat16), "ctx").astype(jnp.float32),
        lax.psum(owned_vb.astype(jnp.bfloat16), "ctx").astype(jnp.float32),
        lax.psum(owned_pw.astype(jnp.bfloat16), "ctx").astype(jnp.float32),
        lax.psum(owned_pb.astype(jnp.bfloat16), "ctx").astype(jnp.float32),
    )
    return (
        out_rows,
        grad_inputs,
        total_g1,
        total_b1,
        total_qkv,
        total_qb,
        total_vb,
        total_pw,
        total_pb,
        total_g2,
        total_b2,
        total_fcw,
        total_fcb,
        total_ow,
        total_ob,
    )


def solution(mesh):
    placed = (
        P(("fsdp", "ctx"), None),
        P(),
        P("fsdp"),
        P("fsdp"),
        P("fsdp", None),
        P("fsdp"),
        P("fsdp"),
        P("fsdp", None),
        P("fsdp"),
        P("fsdp"),
        P("fsdp"),
        P("fsdp", None),
        P("fsdp"),
        P("fsdp", None),
        P("fsdp"),
        P(("fsdp", "ctx"), None),
    )
    return jax.shard_map(
        body,
        mesh=mesh,
        in_specs=placed,
        out_specs=(
            P(("fsdp", "ctx"), None),
            P(("fsdp", "ctx"), None),
            P("fsdp"),
            P("fsdp"),
            P("fsdp", None),
            P("fsdp"),
            P("fsdp"),
            P("fsdp", None),
            P("fsdp"),
            P("fsdp"),
            P("fsdp"),
            P("fsdp", None),
            P("fsdp"),
            P("fsdp", None),
            P("fsdp"),
        ),
        check_vma=False,
    )
```

profile of v0, /device:TPU:0, one launch (start us, length us, event | category | flops | bytes accessed | tf_op | source)
XLA Modules:
  0.0 1569.6 jit_solution(5104515425968146760)
XLA Ops:
  10.6 21.1 %all-reduce.13 = (bf16[1600]{0:T(1024)(128)(2,1)S(1)}, bf16[1600]{0:T(1024)(128)(2,1)S(1)}, bf16[1600]{0:T(1024)(128)(2,1)S(1)}, bf16[1600]{0:T(1024)(128)(2,1)S(1)}, bf16[1600]{0:T(1024)(128)(2,1)S(1)}) all-reduce(bf16[1600]{0:T(1024)(128)(2,1)S(1)} %dynamic-update-slice.2, ...), channel_id=1, replica_groups=mesh['ctx'=8,'fsdp'=4] {'fsdp'}, use_global_device_ids=true, to_apply=%add.2 | all-reduce | flops 8000 | bytes 32000
  32.8 246.5 %all-gather.7.cloned.1.call-done = bf16[1600,4800]{1,0:T(8,128)(2,1)} async-done(((bf16[400,4800]{1,0:T(8,128)(2,1)}), bf16[1600,4800]{1,0:T(8,128)(2,1)}) %all-gather.7.cloned.1.call-update) | async-done | bytes 15360016 | tf_op jit(solution)/shard_map/all_gather | solution.py:55
  279.4 12.1 fusion.80
  299.0 11.7 all_to_all.51
  310.7 5.9 copy.78
  316.8 5.1 all-to-all-start.1
  324.4 8.5 reshape.304
  335.8 19.6 %while.39 = (s32[]{:T(128)}, f32[25,128]{1,0:T(8,128)S(1)}, f32[25,128]{1,0:T(8,128)S(1)}, s32[2,512]{1,0:T(2,128)S(1)}, bf16[2,512,25,64]{1,3,2,0:T(8,128)(2,1)...) while((s32[]{:T(128)}, f32[25,128]{1,0:T(8,128)S(1)}, ...), condition=%wide.region_5.6_spmd.clone, body=%wide.region_2.5_spmd.clone.sunk | while | flops 221265664 | bytes 15526528 | solution.py:98
  336.1 5.2 fusion.175
  345.9 5.2 fusion.175
  355.3 4.9 all-gather.9.cloned.1.call-done
  360.2 8.5 reshape.303
  368.7 4.8 copy.75
  373.5 21.0 %while.40 = (s32[]{:T(128)}, f32[128,25,64]{0,2,1:T(8,128)}, bf16[2,512,25,64]{1,3,2,0:T(8,128)(2,1)}, s32[2,512]{1,0:T(2,128)S(1)}, bf16[2,512,25,64]{1,3,2,0:T...) while((s32[]{:T(128)}, f32[128,25,64]{0,2,1:T(8,128)}, ...), condition=%wide.region_7.8_spmd.clone, body=%wide.region_6.7_spmd.clone.sunk | while | flops 426459264 | bytes 5482114 | solution.py:110
  373.8 4.7 fusion.181
  378.8 5.0 fusion.181
  396.5 129.3 %all-gather.13.cloned.1.call-done = bf16[1600,1600]{1,0:T(8,128)(2,1)} async-done(((bf16[400,1600]{1,0:T(8,128)(2,1)}), bf16[1600,1600]{1,0:T(8,128)(2,1)}) %all-gather.13.cloned.1.call-update) | async-done | bytes 5120016 | tf_op jit(solution)/shard_map/all_gather | solution.py:58
  525.8 5.0 fusion.125
  533.0 31.9 %all-gather.17.cloned.1.call-done = bf16[512,1600]{0,1:T(8,128)(2,1)} async-done(((bf16[128,1600]{0,1:T(8,128)(2,1)}), bf16[512,1600]{0,1:T(8,128)(2,1)}) %all-gather.17.cloned.1.call-update) | async-done | bytes 1638416 | tf_op jit(solution)/shard_map/all_gather | solution.py:135
  564.9 7.9 fusion.126
  572.8 31.1 %all-gather.15.cloned.1.call-done = bf16[512,1600]{0,1:T(8,128)(2,1)} async-done(((bf16[128,1600]{0,1:T(8,128)(2,1)}), bf16[512,1600]{0,1:T(8,128)(2,1)}) %all-gather.15.cloned.1.call-update) | async-done | bytes 1638416 | tf_op jit(solution)/shard_map/all_gather | solution.py:134
  603.9 11.7 fusion.118
  616.8 6.7 convolution_convert_fusion.4
  627.1 35.8 %reduce-scatter.21.cloned.1.call-done = bf16[128,1600]{1,0:T(8,128)(2,1)} async-done(((bf16[512,1600]{1,0:T(8,128)(2,1)}), bf16[128,1600]{1,0:T(8,128)(2,1)}) %reduce-scatter.21.cloned.1.call-update) | async-done | bytes 409616
  675.4 49.1 %while.41 = (s32[]{:T(128)}, f32[128,25,64]{0,2,1:T(8,128)}, bf16[2,512,25,64]{1,3,2,0:T(8,128)(2,1)}, bf16[2,512,25,64]{1,3,2,0:T(8,128)(2,1)}, bf16[2,512,25,6...) while((s32[]{:T(128)}, f32[128,25,64]{0,2,1:T(8,128)}, ...), condition=%wide.region_16.17_spmd.clone, body=%wide.region_15.16_spmd.clone.sunk | while | flops 1068712064 | bytes 150980000 | solution.py:231
  675.8 5.2 fusion.192
  681.3 6.4 fusion.193
  700.1 5.1 fusion.192
  705.5 6.4 fusion.193
  724.5 5.3 copy.82
  750.5 30.1 %reduce-scatter.25.cloned.1.call-done = bf16[128,1600]{1,0:T(8,128)(2,1)} async-done(((bf16[1024,1600]{1,0:T(8,128)(2,1)}), bf16[128,1600]{1,0:T(8,128)(2,1)}) %reduce-scatter.25.cloned.1.call-update) | async-done | bytes 409616
  781.9 50.1 %reduce-scatter.23.cloned.1.call-done = bf16[128,1600]{1,0:T(8,128)(2,1)} async-done(((bf16[1024,1600]{1,0:T(8,128)(2,1)}), bf16[128,1600]{1,0:T(8,128)(2,1)}) %reduce-scatter.23.cloned.1.call-update) | async-done | bytes 409616
  833.4 8.5 convolution_convert_fusion
  843.3 6.3 convolution_convert_fusion.2
  849.6 5.1 all-to-all-start.3
  855.0 8.0 convolution_convert_fusion.5
  866.8 8.1 convolution_convert_fusion.1
  874.9 176.1 %all-to-all-done.3 = bf16[4,400,1600]{2,1,0:T(8,128)(2,1)} async-done(((bf16[4,400,1600]{2,1,0:T(8,128)(2,1)}), bf16[4,400,1600]{2,1,0:T(8,128)(2,1)}, u32[]{:S(2)}, u32[]{:S(2)}) %all-to-all-start.3) | async-done | bytes 5120032 | tf_op jit(solution)/shard_map/all_to_all | solution.py:178
  1051.0 6.9 copy.84
  1057.9 9.8 all_to_all.59
  1067.8 228.2 %reduce-scatter.15.cloned.1.call-done = bf16[400,4800]{1,0:T(8,128)(2,1)} async-done(((bf16[1600,4800]{1,0:T(8,128)(2,1)}), bf16[400,4800]{1,0:T(8,128)(2,1)}) %reduce-scatter.15.cloned.1.call-update) | async-done | bytes 3840016 | tf_op jit(solution)/shard_map/reduce_scatter | solution.py:267
  1301.9 33.4 %reduce-scatter.19.cloned.1.call-done = bf16[128,1600]{1,0:T(8,128)(2,1)} async-done(((bf16[512,1600]{1,0:T(8,128)(2,1)}), bf16[128,1600]{1,0:T(8,128)(2,1)}) %reduce-scatter.19.cloned.1.call-update) | async-done | bytes 409616
  1336.7 9.3 fusion.117
  1346.6 16.9 %all-reduce.12 = (bf16[1600]{0:T(1024)(128)(2,1)S(1)}, bf16[1600]{0:T(1024)(128)(2,1)S(1)}, bf16[1600]{0:T(1024)(128)(2,1)S(1)}, bf16[1600]{0:T(1024)(128)(2,1)S(1)}, bf16[1600]{0:T(1024)(128)(2,1)S(1)}) all-reduce(bf16[1600]{0:T(1024)(128)(2,1)S(1)} %get-tuple-element.374, ...), channel_id=6, replica_groups=mesh['ctx'=8,'fsdp'=4] {'fsdp'}, use_global_device_ids=true, to_apply=%region_22.23.clone | all-reduce | flops 8000 | bytes 32000
  1363.9 24.1 %all-reduce.10 = (bf16[400]{0:T(512)(128)(2,1)S(1)}, bf16[400]{0:T(512)(128)(2,1)S(1)}, bf16[400]{0:T(512)(128)(2,1)S(1)}, bf16[400]{0:T(512)(128)(2,1)S(1)}, bf...) all-reduce(bf16[400]{0:T(512)(128)(2,1)S(1)} %dynamic-slice.6, ...), channel_id=1, replica_groups=mesh['ctx'=8,'fsdp'=4] {'ctx'}, use_global_device_ids=true, to_apply=%region_23.24 | all-reduce | flops 4800 | bytes 19200 | tf_op jit(solution)/shard_map/psum | solution.py:284
  1395.2 150.3 %all-reduce.16.cloned.1.call-done = (bf16[400,4800]{1,0:T(8,128)(2,1)}, bf16[400,1600]{1,0:T(8,128)(2,1)}, bf16[400,6400]{1,0:T(8,128)(2,1)}, bf16[1600,1600]{1,0:T(8,128)(2,1)}) async-done(((bf16[400,4800]{1,0:T(8,128)(2,1)}, bf16[400,1600]{1,0:T(8,128)(2,1)}, bf16[400,6400]{1,0:T(8,128)(2,1)}, bf16[1600,1600]{1,0:T(8,128)(2,1)}), (bf16[400,4800]{1,0:T(8,128)(2,1)}, bf16[400,1600]{1,0:T(8,128)(2,1)}, ...) | async-done | bytes 15360016 | tf_op jit(solution)/shard_map/psum | solution.py:286
  1545.5 6.0 convert_element_type.266
  1557.9 4.8 convert_element_type.281
  (307 shorter events, 122.6 us)
Async XLA Ops:
  7.2 24.6 %copy-start.7 = (bf16[128,1600]{0,1:T(8,128)(2,1)S(1)}, bf16[128,1600]{0,1:T(8,128)(2,1)}, u32[]{:S(2)}) copy-start(bf16[128,1600]{0,1:T(8,128)(2,1)} %param.22) | copy-start | bytes 1228804
  7.3 272.1 %all-gather.7.cloned.1.call-start = ((), (), s32[]{:S(2)}) async-start(), calls=%async_computation.10 | async-start | bytes 19456000 | tf_op jit(solution)/shard_map/all_gather | solution.py:55
  8.0 316.4 %all-gather.11.cloned.1.call-start = ((), (), s32[]{:S(2)}) async-start(), calls=%async_computation.12 | async-start | bytes 3686400 | tf_op jit(solution)/shard_map/all_gather | solution.py:71
  31.7 259.8 %copy-start.28 = (f32[1600]{0:T(1024)}, f32[1600]{0:T(1024)S(1)}, u32[]{:S(2)}) copy-start(f32[1600]{0:T(1024)S(1)} %convert_element_type.230) | copy-start | bytes 19204
  31.8 259.7 %copy-start.30 = (f32[1600]{0:T(1024)}, f32[1600]{0:T(1024)S(1)}, u32[]{:S(2)}) copy-start(f32[1600]{0:T(1024)S(1)} %convert_element_type.231) | copy-start | bytes 19204
  32.1 259.4 %copy-start.33 = (f32[128]{0:T(128)}, f32[128]{0:T(128)S(1)}, u32[]{:S(2)}) copy-start(f32[128]{0:T(128)S(1)} %broadcast_multiply_fusion.2) | copy-start | bytes 1540
  32.8 258.7 %copy-start.35 = (f32[128]{0:T(128)}, f32[128]{0:T(128)S(1)}, u32[]{:S(2)}) copy-start(f32[128]{0:T(128)S(1)} %fusion.110) | copy-start | bytes 1540
  291.6 7.0 copy-start.39
  292.7 67.6 %all-gather.9.cloned.1.call-start = ((), (), s32[]{:S(2)}) async-start(), calls=%async_computation.11 | async-start | bytes 3686400 | tf_op jit(solution)/shard_map/all_gather | solution.py:72
  293.4 232.4 %all-gather.13.cloned.1.call-start = ((), (), s32[]{:S(2)}) async-start(), calls=%async_computation.13 | async-start | bytes 6656000 | tf_op jit(solution)/shard_map/all_gather | solution.py:58
  294.7 22.1 %all-to-all-start = ((bf16[400,4,3]{0,2,1:T(4,128)(2,1)}), bf16[400,4,3]{0,2,1:T(4,128)(2,1)S(1)}, u32[]{:S(2)}, u32[]{:S(2)}) async-start(bf16[400,4,3]{0,2,1:T(4,128)(2,1)} %tile.2), calls=%async_computation | async-start | bytes 32768 | tf_op jit(solution)/shard_map/all_to_all | solution.py:127
  297.9 267.0 %all-gather.17.cloned.1.call-start = ((), (), s32[]{:S(2)}) async-start(), calls=%async_computation.15 | async-start | bytes 2048000 | tf_op jit(solution)/shard_map/all_gather | solution.py:135
  316.8 256.0 %all-to-all-start.1 = ((bf16[400,4,1600]{2,0,1:T(8,128)(2,1)}), bf16[400,4,1600]{2,0,1:T(8,128)(2,1)}, u32[]{:S(2)}, u32[]{:S(2)}) async-start(bf16[400,4,1600]{2,0,1:T(8,128)(2,1)} %copy.78), calls=%async_computation.1 | async-start | bytes 10649600 | tf_op jit(solution)/shard_map/all_to_all | solution.py:126
  321.9 282.0 %all-gather.15.cloned.1.call-start = ((), (), s32[]{:S(2)}) async-start(), calls=%async_computation.14 | async-start | bytes 2048000 | tf_op jit(solution)/shard_map/all_gather | solution.py:134
  525.8 7.2 copy-start.37
  532.9 130.0 %reduce-scatter.21.cloned.1.call-start = ((), (), s32[]{:S(2)}) async-start(), calls=%async_computation.19 | async-start | bytes 2129920
  627.1 153.6 %reduce-scatter.25.cloned.1.call-start = ((), (), s32[]{:S(2)}) async-start(), calls=%async_computation.21 | async-start | bytes 3833856
  675.8 5.2 copy-start
  692.3 6.0 copy-start.13
  700.1 5.2 copy-start
  712.0 4.8 copy-start.15
  716.8 6.0 copy-start.13
  734.3 97.8 %reduce-scatter.23.cloned.1.call-start = ((), (), s32[]{:S(2)}) async-start(), calls=%async_computation.20 | async-start | bytes 3833856
  744.0 323.8 %reduce-scatter.17.cloned.1.call-start = ((), (), s32[]{:S(2)}) async-start(), calls=%async_computation.17 | async-start | bytes 6656000 | tf_op jit(solution)/shard_map/reduce_scatter | solution.py:276
  749.1 84.2 %copy-start.8 = (bf16[128,1600]{0,1:T(8,128)(2,1)S(1)}, bf16[128,1600]{0,1:T(8,128)(2,1)}, u32[]{:S(2)}) copy-start(bf16[128,1600]{0,1:T(8,128)(2,1)} %param.22) | copy-start | bytes 1228804
  749.1 84.2 %copy-start.29 = (f32[1600]{0:T(1024)S(1)}, f32[1600]{0:T(1024)}, u32[]{:S(2)}) copy-start(f32[1600]{0:T(1024)} %copy-done.28) | copy-start | bytes 19204
  749.1 84.2 %copy-start.31 = (f32[1600]{0:T(1024)S(1)}, f32[1600]{0:T(1024)}, u32[]{:S(2)}) copy-start(f32[1600]{0:T(1024)} %copy-done.30) | copy-start | bytes 19204
  749.1 84.2 %copy-start.34 = (f32[128]{0:T(128)S(1)}, f32[128]{0:T(128)}, u32[]{:S(2)}) copy-start(f32[128]{0:T(128)} %copy-done.33) | copy-start | bytes 1540
  749.1 84.2 %copy-start.36 = (f32[128]{0:T(128)S(1)}, f32[128]{0:T(128)}, u32[]{:S(2)}) copy-start(f32[128]{0:T(128)} %copy-done.35) | copy-start | bytes 1540
  749.1 546.8 %reduce-scatter.15.cloned.1.call-start = ((), (), s32[]{:S(2)}) async-start(), calls=%async_computation.16 | async-start | bytes 19456000 | tf_op jit(solution)/shard_map/reduce_scatter | solution.py:267
  750.5 91.3 %copy-start.21 = (bf16[128,25,64]{0,2,1:T(8,128)(2,1)}, bf16[128,25,64]{0,2,1:T(8,128)(2,1)S(1)}, u32[]{:S(2)}) copy-start(bf16[128,25,64]{0,2,1:T(8,128)(2,1)S(1)} %get-tuple-element.465) | copy-start | bytes 1228804
  781.9 59.9 %copy-start.22 = (bf16[128,1600]{0,1:T(8,128)(2,1)}, bf16[128,1600]{0,1:T(8,128)(2,1)S(1)}, u32[]{:S(2)}) copy-start(bf16[128,1600]{0,1:T(8,128)(2,1)S(1)} %copy.96) | copy-start | bytes 1228804
  833.3 8.5 copy-start.23
  849.6 201.4 %all-to-all-start.3 = ((bf16[4,400,1600]{2,1,0:T(8,128)(2,1)}), bf16[4,400,1600]{2,1,0:T(8,128)(2,1)}, u32[]{:S(2)}, u32[]{:S(2)}) async-start(bf16[4,400,1600]{2,1,0:T(8,128)(2,1)} %bitcast.213), calls=%async_computation.5 | async-start | bytes 10649600 | tf_op jit(solution)/shard_map/all_to_all | solution.py:178
  854.7 480.5 %reduce-scatter.19.cloned.1.call-start = ((), (), s32[]{:S(2)}) async-start(), calls=%async_computation.18 | async-start | bytes 2129920
  866.7 678.8 %all-reduce.16.cloned.1.call-start = ((), (), s32[]{:S(2)}) async-start(), calls=%async_computation.22 | async-start | bytes 31334400 | tf_op jit(solution)/shard_map/psum | solution.py:286
  1296.0 40.5 %copy-start.19 = (bf16[128,1600]{1,0:T(8,128)(2,1)S(1)}, bf16[128,1600]{1,0:T(8,128)(2,1)}, u32[]{:S(2)}) copy-start(bf16[128,1600]{1,0:T(8,128)(2,1)} %reduce-scatter.25.cloned.1.call-done) | copy-start | bytes 1228804
  1297.9 38.6 %all-to-all-start.2 = ((bf16[4,400,2]{1,2,0:T(2,128)(2,1)}), bf16[4,400,2]{1,2,0:T(2,128)(2,1)S(1)}, u32[]{:S(2)}, u32[]{:S(2)}) async-start(bf16[4,400,2]{1,2,0:T(2,128)(2,1)} %copy.83), calls=%async_computation.4 | async-start | bytes 16384 | tf_op jit(solution)/shard_map/all_to_all | solution.py:181
  1336.6 9.4 copy-start.50
  1336.6 27.3 %copy-start.38 = (bf16[1600]{0:T(1024)(128)(2,1)S(1)}, bf16[1600]{0:T(1024)(128)(2,1)}, u32[]{:S(2)}) copy-start(bf16[1600]{0:T(1024)(128)(2,1)} %get-tuple-element.460) | copy-start | bytes 9604
  1336.6 56.7 %copy-start.5 = (f32[128,1600]{0,1:T(8,128)S(1)}, f32[128,1600]{0,1:T(8,128)}, u32[]{:S(2)}) copy-start(f32[128,1600]{0,1:T(8,128)} %copy-done.4) | copy-start | bytes 2457604
  1336.6 56.7 %copy-start.9 = (bf16[128,1600]{0,1:T(8,128)(2,1)S(1)}, bf16[128,1600]{0,1:T(8,128)(2,1)}, u32[]{:S(2)}) copy-start(bf16[128,1600]{0,1:T(8,128)(2,1)} %copy.92) | copy-start | bytes 1228804
  1336.7 56.7 %copy-start.11 = (bf16[128,1600]{0,1:T(8,128)(2,1)S(1)}, bf16[128,1600]{0,1:T(8,128)(2,1)}, u32[]{:S(2)}) copy-start(bf16[128,1600]{0,1:T(8,128)(2,1)} %param.37) | copy-start | bytes 1228804
  1336.7 56.6 %copy-start.32 = (f32[1600]{0:T(1024)S(1)}, f32[1600]{0:T(1024)}, u32[]{:S(2)}) copy-start(f32[1600]{0:T(1024)} %get-tuple-element.378) | copy-start | bytes 19204
  1545.5 7.6 slice-start.2
  1545.5 6.0 copy-start.26
  1545.5 7.6 slice-start.3
  1551.5 6.4 slice-start
  (34 other events, 89.3 us)
Sparse Core Ops, SparseCore 0:
  9.6 269.6 all-gather.6
  292.8 31.6 all-gather.10
  326.9 33.2 all-gather.8
  361.7 164.0 all-gather.12
  527.2 37.6 all-gather.16
  566.9 36.9 all-gather.14
  627.2 35.6 reduce-scatter.20
  734.4 46.2 reduce-scatter.24
  784.7 47.3 reduce-scatter.22
  834.8 164.3 reduce-scatter.16
  1001.5 294.3 reduce-scatter.14
  1298.7 36.4 reduce-scatter.18
  1339.8 205.6 all-reduce.15
where the time goes:
time: 1580 us; the launch traced here: 1570 us
  waiting for transfers between devices  1150 us (73%)
  matrix products  151 us (10%)
  local copies, waits for them, and re-layouts  113 us (7%)
  blocking collectives  62.2 us (4%)
  other arithmetic  45.8 us (3%)
  starting transfers between devices  18.1 us (1%)
  between operations  16.5 us (1%)
    all_gather x1, waiting for transfers between devices, body(): lax.all_gather(qkv_weight, 'fsdp', axis=0, tiled=True)  247 us
    reduce_scatter x1, waiting for transfers between devices, body(): lax.psum_scatter(grad_qkv_w.astype(jnp.bfloat16), 'fsdp', scatter_dimensi...  228 us
    all_to_all x1, waiting for transfers between devices, body(): lax.all_to_all(grad_fc_cols.astype(jnp.bfloat16), 'fsdp', split_axis=0, c...  176 us
    unnamed x17, waiting for transfers between devices  152 us
    psum x1, waiting for transfers between devices, body(): lax.psum(owned_qkv.astype(jnp.bfloat16), 'ctx').astype(jnp.float32)  150 us
    all_gather x1, waiting for transfers between devices, body(): lax.all_gather(proj_weight, 'fsdp', axis=0, tiled=True)  129 us
    unnamed x127, local copies, waits for them, and re-layouts  40.2 us
    unnamed x2, blocking collectives  38 us
  transfers between devices with their start and end apart: 17, of which 13 were waited for; matrix products, arithmetic and copies ran while one was open for 10% of the time, Pallas kernels for 0%

commit v1 on v0

--- a/solution.py
+++ b/solution.py
@@ -5,6 +5,19 @@
 from jax.sharding import PartitionSpec as P
 
 HEADS = 25
+
+
+def collect(shard, axis, dim):
+    ways = lax.axis_size(axis)
+    up = [(d, (d + 1) % ways) for d in range(ways)]
+    down = [(d, (d - 1) % ways) for d in range(ways)]
+    earlier, later = ([shard], [shard])
+    for _ in range(ways // 2):
+        earlier.append(lax.ppermute(earlier[-1], axis, up))
+    for _ in range((ways - 1) // 2):
+        later.append(lax.ppermute(later[-1], axis, down))
+    line = jnp.concatenate([*earlier[::-1], *later[1:]], axis=dim)
+    return jnp.roll(line, (lax.axis_index(axis) - ways // 2) * shard.shape[dim], axis=dim)
 
 
 def layer_norm(values, gain_vec, shift_vec):
@@ -55,7 +68,7 @@
         lax.all_gather(qkv_weight, "fsdp", axis=0, tiled=True),
         lax.all_gather(query_bias, "fsdp", axis=0, tiled=True),
         lax.all_gather(value_bias, "fsdp", axis=0, tiled=True),
-        lax.all_gather(proj_weight, "fsdp", axis=0, tiled=True),
+        collect(proj_weight, "fsdp", 0),
         lax.all_gather(proj_bias, "fsdp", axis=0, tiled=True),
     )
     inputs = tokens.astype(jnp.float32)

time: 1580 us -> 1530 us (0.968)
  waiting for transfers between devices: 1150 us -> 1090 us
    all_gather x1 -> x0, waiting for transfers between devices: 129 us -> none  [body(): lax.all_gather(proj_weight, 'fsdp', axis=0, tiled=True)]
    all_to_all x1, waiting for transfers between devices: 0.01 us -> 52.7 us  [body(): lax.all_to_all(small_tiled, 'fsdp', split_axis=1, concat_axis=0, tiled=True)]
    all_to_all x1, waiting for transfers between devices: 0.01 us -> 46.7 us  [body(): lax.all_to_all(fc_weight, 'fsdp', split_axis=1, concat_axis=0, tiled=True)]
    ppermute x0 -> x3, waiting for transfers between devices: none -> 32.9 us  [the longest x2 32.9 us: collect(): earlier.append(lax.ppermute(earlier[-1], axis, up))]
    all_gather x1, waiting for transfers between devices: 31.9 us -> 0.02 us  [body(): lax.all_gather(cotangent, 'fsdp', axis=0, tiled=True)]
    all_gather x1, waiting for transfers between devices: 31.1 us -> 0.01 us  [body(): lax.all_gather(normed_two, 'fsdp', axis=0, tiled=True)]
    unnamed x127 -> x134, local copies, waits for them, and re-layouts: 40.2 us -> 51.1 us
    unnamed x17 -> x16, waiting for transfers between devices: 152 us -> 151 us
  transfers between devices with their start and end apart: 17 -> 19, of which waited for: 13 -> 11; matrix products, arithmetic and copies ran while one was open for 10% -> 11% of each run, Pallas kernels for 0% -> 0%
where the time goes in v1:
time: 1530 us; the launch traced here: 1520 us
  waiting for transfers between devices  1090 us (71%)
  matrix products  155 us (10%)
  local copies, waits for them, and re-layouts  118 us (8%)
  blocking collectives  62.2 us (4%)
  other arithmetic  45.4 us (3%)
  starting transfers between devices  22 us (1%)
  between operations  16.8 us (1%)
    all_gather x1, waiting for transfers between devices, body(): lax.all_gather(qkv_weight, 'fsdp', axis=0, tiled=True)  247 us
    reduce_scatter x1, waiting for transfers between devices, body(): lax.psum_scatter(grad_qkv_w.astype(jnp.bfloat16), 'fsdp', scatter_dimensi...  228 us
    all_to_all x1, waiting for transfers between devices, body(): lax.all_to_all(grad_fc_cols.astype(jnp.bfloat16), 'fsdp', split_axis=0, c...  176 us
    unnamed x16, waiting for transfers between devices  151 us
    psum x1, waiting for transfers between devices, body(): lax.psum(owned_qkv.astype(jnp.bfloat16), 'ctx').astype(jnp.float32)  150 us
    all_to_all x1, waiting for transfers between devices, body(): lax.all_to_all(small_tiled, 'fsdp', split_axis=1, concat_axis=0, tiled=True)  52.7 us
    unnamed x134, local copies, waits for them, and re-layouts  51.1 us
    all_to_all x1, waiting for transfers between devices, body(): lax.all_to_all(fc_weight, 'fsdp', split_axis=1, concat_axis=0, tiled=True)  46.7 us
  transfers between devices with their start and end apart: 19, of which 11 were waited for; matrix products, arithmetic and copies ran while one was open for 11% of the time, Pallas kernels for 0%

profile of v1, /device:TPU:0, one launch (start us, length us, event | category | flops | bytes accessed | tf_op | source)
XLA Modules:
  0.0 1516.6 jit_solution(18275562951909616848)
XLA Ops:
  10.6 21.1 %all-reduce.13 = (bf16[1600]{0:T(1024)(128)(2,1)S(1)}, bf16[1600]{0:T(1024)(128)(2,1)S(1)}, bf16[1600]{0:T(1024)(128)(2,1)S(1)}, bf16[1600]{0:T(1024)(128)(2,1)S(1)}, bf16[1600]{0:T(1024)(128)(2,1)S(1)}) all-reduce(bf16[1600]{0:T(1024)(128)(2,1)S(1)} %dynamic-update-slice.2, ...), channel_id=1, replica_groups=mesh['ctx'=8,'fsdp'=4] {'fsdp'}, use_global_device_ids=true, to_apply=%add.2 | all-reduce | flops 8000 | bytes 32000
  32.3 247.1 %all-gather.6.cloned.1.call-done = bf16[1600,4800]{1,0:T(8,128)(2,1)} async-done(((bf16[400,4800]{1,0:T(8,128)(2,1)}), bf16[1600,4800]{1,0:T(8,128)(2,1)}) %all-gather.6.cloned.1.call-update) | async-done | bytes 15360016 | tf_op jit(solution)/shard_map/all_gather | solution.py:68
  279.4 12.1 fusion.80
  293.5 32.9 %collective-permute-done = bf16[400,1600]{1,0:T(8,128)(2,1)S(1)} collective-permute-done((bf16[400,1600]{1,0:T(8,128)(2,1)S(1)}, bf16[400,1600]{1,0:T(8,128)(2,1)S(1)}, u32[]{:S(2)}, u32[]{:S(2)}) %collective-permute-start) | collective-permute-done | bytes 1280032 | tf_op jit(solution)/shard_map/ppermute | solution.py:16
  335.2 11.7 all_to_all.51
  346.9 5.7 copy.78
  352.8 52.7 %all-to-all-done = bf16[400,4,3]{0,2,1:T(4,128)(2,1)S(1)} async-done(((bf16[400,4,3]{0,2,1:T(4,128)(2,1)}), bf16[400,4,3]{0,2,1:T(4,128)(2,1)S(1)}, u32[]{:S(2)}, u32[]{:S(2)}) %all-to-all-start) | async-done | bytes 9632 | tf_op jit(solution)/shard_map/all_to_all | solution.py:140
  405.6 5.1 all-to-all-start.1
  426.0 8.5 reshape.304
  437.1 19.6 %while.39 = (s32[]{:T(128)}, f32[25,128]{1,0:T(8,128)S(1)}, f32[25,128]{1,0:T(8,128)S(1)}, s32[2,512]{1,0:T(2,128)S(1)}, bf16[2,512,25,64]{1,3,2,0:T(8,128)(2,1)...) while((s32[]{:T(128)}, f32[25,128]{1,0:T(8,128)S(1)}, ...), condition=%wide.region_5.6_spmd.clone, body=%wide.region_2.5_spmd.clone.sunk | while | flops 221265664 | bytes 15526520 | solution.py:111
  437.5 5.2 fusion.187
  447.3 5.2 fusion.187
  456.7 8.5 reshape.303
  465.2 4.4 copy.75
  469.6 21.5 %while.40 = (s32[]{:T(128)}, f32[128,25,64]{0,2,1:T(8,128)}, bf16[2,512,25,64]{1,3,2,0:T(8,128)(2,1)}, s32[2,512]{1,0:T(2,128)S(1)}, bf16[2,512,25,64]{1,3,2,0:T...) while((s32[]{:T(128)}, f32[128,25,64]{0,2,1:T(8,128)}, ...), condition=%wide.region_7.8_spmd.clone, body=%wide.region_6.7_spmd.clone.sunk | while | flops 426459264 | bytes 5481595 | solution.py:123
  470.0 4.7 fusion.193
  475.0 5.0 fusion.193
  492.4 5.2 fusion.139
  499.8 7.9 fusion.140
  507.7 46.7 %all-to-all-done.1 = bf16[400,4,1600]{2,0,1:T(8,128)(2,1)} async-done(((bf16[400,4,1600]{2,0,1:T(8,128)(2,1)}), bf16[400,4,1600]{2,0,1:T(8,128)(2,1)}, u32[]{:S(2)}, u32[]{:S(2)}) %all-to-all-start.1) | async-done | bytes 5120032 | tf_op jit(solution)/shard_map/all_to_all | solution.py:139
  554.3 11.7 fusion.132
  567.2 6.7 convolution_convert_fusion.4
  577.6 35.7 %reduce-scatter.21.cloned.1.call-done = bf16[128,1600]{1,0:T(8,128)(2,1)} async-done(((bf16[512,1600]{1,0:T(8,128)(2,1)}), bf16[128,1600]{1,0:T(8,128)(2,1)}) %reduce-scatter.21.cloned.1.call-update) | async-done | bytes 409616
  620.7 4.3 fusion.98
  625.7 44.8 %while.41 = (s32[]{:T(128)}, f32[128,25,64]{0,2,1:T(8,128)}, bf16[2,512,25,64]{1,3,2,0:T(8,128)(2,1)}, bf16[2,512,25,64]{1,3,2,0:T(8,128)(2,1)}, bf16[2,512,25,6...) while((s32[]{:T(128)}, f32[128,25,64]{0,2,1:T(8,128)}, ...), condition=%wide.region_16.17_spmd.clone, body=%wide.region_15.16_spmd.clone.sunk | while | flops 1068712064 | bytes 98549520 | solution.py:244
  626.1 5.2 fusion.204
  631.7 6.4 fusion.205
  648.2 5.1 fusion.204
  653.6 6.4 fusion.205
  670.6 5.3 copy.81
  696.6 30.1 %reduce-scatter.23.cloned.1.call-done = bf16[128,1600]{1,0:T(8,128)(2,1)} async-done(((bf16[1024,1600]{1,0:T(8,128)(2,1)}), bf16[128,1600]{1,0:T(8,128)(2,1)}) %reduce-scatter.23.cloned.1.call-update) | async-done | bytes 409616
  728.0 50.1 %reduce-scatter.25.cloned.1.call-done = bf16[128,1600]{1,0:T(8,128)(2,1)} async-done(((bf16[1024,1600]{1,0:T(8,128)(2,1)}), bf16[128,1600]{1,0:T(8,128)(2,1)}) %reduce-scatter.25.cloned.1.call-update) | async-done | bytes 409616
  779.4 8.4 convolution_convert_fusion
  789.4 6.3 convolution_convert_fusion.2
  795.7 5.1 all-to-all-start.3
  801.1 8.0 convolution_convert_fusion.5
  812.8 8.1 convolution_convert_fusion.1
  821.0 176.4 %all-to-all-done.3 = bf16[4,400,1600]{2,1,0:T(8,128)(2,1)} async-done(((bf16[4,400,1600]{2,1,0:T(8,128)(2,1)}), bf16[4,400,1600]{2,1,0:T(8,128)(2,1)}, u32[]{:S(2)}, u32[]{:S(2)}) %all-to-all-start.3) | async-done | bytes 5120032 | tf_op jit(solution)/shard_map/all_to_all | solution.py:191
  997.4 6.9 copy.84
  1004.3 9.8 all_to_all.59
  1014.1 228.1 %reduce-scatter.15.cloned.1.call-done = bf16[400,4800]{1,0:T(8,128)(2,1)} async-done(((bf16[1600,4800]{1,0:T(8,128)(2,1)}), bf16[400,4800]{1,0:T(8,128)(2,1)}) %reduce-scatter.15.cloned.1.call-update) | async-done | bytes 3840016 | tf_op jit(solution)/shard_map/reduce_scatter | solution.py:280
  1248.0 33.6 %reduce-scatter.19.cloned.1.call-done = bf16[128,1600]{1,0:T(8,128)(2,1)} async-done(((bf16[512,1600]{1,0:T(8,128)(2,1)}), bf16[128,1600]{1,0:T(8,128)(2,1)}) %reduce-scatter.19.cloned.1.call-update) | async-done | bytes 409616
  1283.1 9.3 fusion.131
  1293.0 16.9 %all-reduce.12 = (bf16[1600]{0:T(1024)(128)(2,1)S(1)}, bf16[1600]{0:T(1024)(128)(2,1)S(1)}, bf16[1600]{0:T(1024)(128)(2,1)S(1)}, bf16[1600]{0:T(1024)(128)(2,1)S(1)}, bf16[1600]{0:T(1024)(128)(2,1)S(1)}) all-reduce(bf16[1600]{0:T(1024)(128)(2,1)S(1)} %get-tuple-element.374, ...), channel_id=6, replica_groups=mesh['ctx'=8,'fsdp'=4] {'fsdp'}, use_global_device_ids=true, to_apply=%region_22.23.clone | all-reduce | flops 8000 | bytes 32000
  1310.3 24.1 %all-reduce.10 = (bf16[400]{0:T(512)(128)(2,1)S(1)}, bf16[400]{0:T(512)(128)(2,1)S(1)}, bf16[400]{0:T(512)(128)(2,1)S(1)}, bf16[400]{0:T(512)(128)(2,1)S(1)}, bf...) all-reduce(bf16[400]{0:T(512)(128)(2,1)S(1)} %dynamic-slice.6, ...), channel_id=1, replica_groups=mesh['ctx'=8,'fsdp'=4] {'ctx'}, use_global_device_ids=true, to_apply=%region_23.24 | all-reduce | flops 4800 | bytes 19200 | tf_op jit(solution)/shard_map/psum | solution.py:297
  1341.7 150.1 %all-reduce.16.cloned.1.call-done = (bf16[400,4800]{1,0:T(8,128)(2,1)}, bf16[400,1600]{1,0:T(8,128)(2,1)}, bf16[400,6400]{1,0:T(8,128)(2,1)}, bf16[1600,1600]{1,0:T(8,128)(2,1)}) async-done(((bf16[400,4800]{1,0:T(8,128)(2,1)}, bf16[400,1600]{1,0:T(8,128)(2,1)}, bf16[400,6400]{1,0:T(8,128)(2,1)}, bf16[1600,1600]{1,0:T(8,128)(2,1)}), (bf16[400,4800]{1,0:T(8,128)(2,1)}, bf16[400,1600]{1,0:T(8,128)(2,1)}, ...) | async-done | bytes 15360016 | tf_op jit(solution)/shard_map/psum | solution.py:299
  1491.8 7.5 convert_element_type.281
  1499.3 4.7 convert_element_type.278
  (300 shorter events, 127.7 us)
Async XLA Ops:
  7.2 24.6 %copy-start.7 = (bf16[128,1600]{0,1:T(8,128)(2,1)S(1)}, bf16[128,1600]{0,1:T(8,128)(2,1)}, u32[]{:S(2)}) copy-start(bf16[128,1600]{0,1:T(8,128)(2,1)} %param.22) | copy-start | bytes 1228804
  7.3 272.1 %all-gather.6.cloned.1.call-start = ((), (), s32[]{:S(2)}) async-start(), calls=%async_computation.10 | async-start | bytes 19456000 | tf_op jit(solution)/shard_map/all_gather | solution.py:68
  8.0 418.0 %all-gather.10.cloned.1.call-start = ((), (), s32[]{:S(2)}) async-start(), calls=%async_computation.12 | async-start | bytes 3686400 | tf_op jit(solution)/shard_map/all_gather | solution.py:84
  31.8 247.6 %copy-start.28 = (f32[1600]{0:T(1024)}, f32[1600]{0:T(1024)S(1)}, u32[]{:S(2)}) copy-start(f32[1600]{0:T(1024)S(1)} %convert_element_type.230) | copy-start | bytes 19204
  31.8 247.6 %copy-start.30 = (f32[1600]{0:T(1024)}, f32[1600]{0:T(1024)S(1)}, u32[]{:S(2)}) copy-start(f32[1600]{0:T(1024)S(1)} %convert_element_type.231) | copy-start | bytes 19204
  32.1 247.3 %copy-start.33 = (f32[128]{0:T(128)}, f32[128]{0:T(128)S(1)}, u32[]{:S(2)}) copy-start(f32[128]{0:T(128)S(1)} %broadcast_multiply_fusion.2) | copy-start | bytes 1540
  32.3 247.1 %copy-start.49 = (f32[128]{0:T(128)}, f32[128]{0:T(128)S(1)}, u32[]{:S(2)}) copy-start(f32[128]{0:T(128)S(1)} %fusion.114) | copy-start | bytes 1540
  32.3 247.1 %copy-start.35 = (f32[128]{0:T(128)}, f32[128]{0:T(128)S(1)}, u32[]{:S(2)}) copy-start(f32[128]{0:T(128)S(1)} %fusion.124) | copy-start | bytes 1540
  291.6 38.7 %copy-start.41 = (bf16[400]{0:T(512)(128)(2,1)S(1)}, bf16[400]{0:T(512)(128)(2,1)}, u32[]{:S(2)}) copy-start(bf16[400]{0:T(512)(128)(2,1)} %param.31) | copy-start | bytes 2404
  291.6 38.7 %copy-start.42 = (bf16[400]{0:T(512)(128)(2,1)S(1)}, bf16[400]{0:T(512)(128)(2,1)}, u32[]{:S(2)}) copy-start(bf16[400]{0:T(512)(128)(2,1)} %param.32) | copy-start | bytes 2404
  291.6 38.7 %copy-start.43 = (bf16[400]{0:T(512)(128)(2,1)S(1)}, bf16[400]{0:T(512)(128)(2,1)}, u32[]{:S(2)}) copy-start(bf16[400]{0:T(512)(128)(2,1)} %param.36) | copy-start | bytes 2404
  291.6 43.2 %copy-start.39 = (s32[8,2]{0,1:T(2,128)S(1)}, s32[8,2]{0,1:T(2,128)}, u32[]{:S(2)}) copy-start(s32[8,2]{0,1:T(2,128)} %param.23) | copy-start | bytes 196
  292.7 164.0 %all-gather.8.cloned.1.call-start = ((), (), s32[]{:S(2)}) async-start(), calls=%async_computation.11 | async-start | bytes 3686400 | tf_op jit(solution)/shard_map/all_gather | solution.py:85
  293.5 33.0 %collective-permute-start = (bf16[400,1600]{1,0:T(8,128)(2,1)S(1)}, bf16[400,1600]{1,0:T(8,128)(2,1)S(1)}, u32[]{:S(2)}, u32[]{:S(2)}) collective-permute-start(bf16[400,1600]{1,0:T(8,128)(2,1)S(1)} %copy-done.12), channel_id=1, source_target_pairs={{0,1},{1,2},{2,3},{3,0},{4,5},{5,6},{6,7},{7,4},{8,9},{9,10},{10,1... | collective-permute-start | bytes 3840008 | tf_op jit(solution)/shard_map/ppermute | solution.py:16
  326.4 85.0 %collective-permute-start.1 = (bf16[400,1600]{1,0:T(8,128)(2,1)S(1)}, bf16[400,1600]{1,0:T(8,128)(2,1)}, u32[]{:S(2)}, u32[]{:S(2)}) collective-permute-start(bf16[400,1600]{1,0:T(8,128)(2,1)S(1)} %collective-permute-done), channel_id=1, source_target_pairs={{0,1},{1,2},{2,3},{3,0},{4,5},{5,6},{6,7},{7,4},{8,9},{9,10},{10,1... | collective-permute-start | bytes 3840008 | tf_op jit(solution)/shard_map/ppermute | solution.py:16
  326.4 89.8 %collective-permute-start.2 = (bf16[400,1600]{1,0:T(8,128)(2,1)S(1)}, bf16[400,1600]{1,0:T(8,128)(2,1)}, u32[]{:S(2)}, u32[]{:S(2)}) collective-permute-start(bf16[400,1600]{1,0:T(8,128)(2,1)S(1)} %copy-done.12), channel_id=1, source_target_pairs={{0,3},{1,0},{2,1},{3,2},{4,7},{5,4},{6,5},{7,6},{8,11},{9,8},{10,9... | collective-permute-start | bytes 3840008 | tf_op jit(solution)/shard_map/ppermute | solution.py:18
  330.9 74.6 %all-to-all-start = ((bf16[400,4,3]{0,2,1:T(4,128)(2,1)}), bf16[400,4,3]{0,2,1:T(4,128)(2,1)S(1)}, u32[]{:S(2)}, u32[]{:S(2)}) async-start(bf16[400,4,3]{0,2,1:T(4,128)(2,1)} %tile.2), calls=%async_computation | async-start | bytes 32768 | tf_op jit(solution)/shard_map/all_to_all | solution.py:140
  334.2 165.6 %all-gather.14.cloned.1.call-start = ((), (), s32[]{:S(2)}) async-start(), calls=%async_computation.14 | async-start | bytes 2048000 | tf_op jit(solution)/shard_map/all_gather | solution.py:148
  405.6 148.8 %all-to-all-start.1 = ((bf16[400,4,1600]{2,0,1:T(8,128)(2,1)}), bf16[400,4,1600]{2,0,1:T(8,128)(2,1)}, u32[]{:S(2)}, u32[]{:S(2)}) async-start(bf16[400,4,1600]{2,0,1:T(8,128)(2,1)} %copy.78), calls=%async_computation.1 | async-start | bytes 10649600 | tf_op jit(solution)/shard_map/all_to_all | solution.py:139
  410.6 143.7 %all-gather.12.cloned.1.call-start = ((), (), s32[]{:S(2)}) async-start(), calls=%async_computation.13 | async-start | bytes 2048000 | tf_op jit(solution)/shard_map/all_gather | solution.py:147
  492.3 7.4 copy-start.37
  499.7 113.5 %reduce-scatter.21.cloned.1.call-start = ((), (), s32[]{:S(2)}) async-start(), calls=%async_computation.18 | async-start | bytes 2129920
  577.5 149.2 %reduce-scatter.23.cloned.1.call-start = ((), (), s32[]{:S(2)}) async-start(), calls=%async_computation.19 | async-start | bytes 3833856
  631.6 6.5 copy-start.3
  653.6 6.5 copy-start.3
  680.3 97.8 %reduce-scatter.25.cloned.1.call-start = ((), (), s32[]{:S(2)}) async-start(), calls=%async_computation.20 | async-start | bytes 3833856
  690.0 324.1 %reduce-scatter.17.cloned.1.call-start = ((), (), s32[]{:S(2)}) async-start(), calls=%async_computation.16 | async-start | bytes 6656000 | tf_op jit(solution)/shard_map/reduce_scatter | solution.py:289
  695.1 84.2 %copy-start.8 = (bf16[128,1600]{0,1:T(8,128)(2,1)S(1)}, bf16[128,1600]{0,1:T(8,128)(2,1)}, u32[]{:S(2)}) copy-start(bf16[128,1600]{0,1:T(8,128)(2,1)} %param.22) | copy-start | bytes 1228804
  695.1 84.3 %copy-start.29 = (f32[1600]{0:T(1024)S(1)}, f32[1600]{0:T(1024)}, u32[]{:S(2)}) copy-start(f32[1600]{0:T(1024)} %copy-done.28) | copy-start | bytes 19204
  695.1 84.3 %copy-start.31 = (f32[1600]{0:T(1024)S(1)}, f32[1600]{0:T(1024)}, u32[]{:S(2)}) copy-start(f32[1600]{0:T(1024)} %copy-done.30) | copy-start | bytes 19204
  695.1 84.3 %copy-start.34 = (f32[128]{0:T(128)S(1)}, f32[128]{0:T(128)}, u32[]{:S(2)}) copy-start(f32[128]{0:T(128)} %copy-done.33) | copy-start | bytes 1540
  695.1 84.3 %copy-start.36 = (f32[128]{0:T(128)S(1)}, f32[128]{0:T(128)}, u32[]{:S(2)}) copy-start(f32[128]{0:T(128)} %copy-done.35) | copy-start | bytes 1540
  695.2 547.0 %reduce-scatter.15.cloned.1.call-start = ((), (), s32[]{:S(2)}) async-start(), calls=%async_computation.15 | async-start | bytes 19456000 | tf_op jit(solution)/shard_map/reduce_scatter | solution.py:280
  696.6 91.3 %copy-start.21 = (bf16[128,25,64]{0,2,1:T(8,128)(2,1)}, bf16[128,25,64]{0,2,1:T(8,128)(2,1)S(1)}, u32[]{:S(2)}) copy-start(bf16[128,25,64]{0,2,1:T(8,128)(2,1)S(1)} %get-tuple-element.465) | copy-start | bytes 1228804
  728.0 59.9 %copy-start.22 = (bf16[128,1600]{0,1:T(8,128)(2,1)}, bf16[128,1600]{0,1:T(8,128)(2,1)S(1)}, u32[]{:S(2)}) copy-start(bf16[128,1600]{0,1:T(8,128)(2,1)S(1)} %copy.94) | copy-start | bytes 1228804
  779.4 8.5 copy-start.23
  795.7 201.7 %all-to-all-start.3 = ((bf16[4,400,1600]{2,1,0:T(8,128)(2,1)}), bf16[4,400,1600]{2,1,0:T(8,128)(2,1)}, u32[]{:S(2)}, u32[]{:S(2)}) async-start(bf16[4,400,1600]{2,1,0:T(8,128)(2,1)} %bitcast.209), calls=%async_computation.5 | async-start | bytes 10649600 | tf_op jit(solution)/shard_map/all_to_all | solution.py:191
  800.8 480.8 %reduce-scatter.19.cloned.1.call-start = ((), (), s32[]{:S(2)}) async-start(), calls=%async_computation.17 | async-start | bytes 2129920
  812.8 679.0 %all-reduce.16.cloned.1.call-start = ((), (), s32[]{:S(2)}) async-start(), calls=%async_computation.21 | async-start | bytes 31334400 | tf_op jit(solution)/shard_map/psum | solution.py:299
  1242.2 40.7 %copy-start.19 = (bf16[128,1600]{1,0:T(8,128)(2,1)S(1)}, bf16[128,1600]{1,0:T(8,128)(2,1)}, u32[]{:S(2)}) copy-start(bf16[128,1600]{1,0:T(8,128)(2,1)} %reduce-scatter.25.cloned.1.call-done) | copy-start | bytes 1228804
  1244.0 38.8 %all-to-all-start.2 = ((bf16[4,400,2]{1,2,0:T(2,128)(2,1)}), bf16[4,400,2]{1,2,0:T(2,128)(2,1)S(1)}, u32[]{:S(2)}, u32[]{:S(2)}) async-start(bf16[4,400,2]{1,2,0:T(2,128)(2,1)} %copy.83), calls=%async_computation.4 | async-start | bytes 16384 | tf_op jit(solution)/shard_map/all_to_all | solution.py:194
  1283.0 9.4 copy-start.50
  1283.0 27.3 %copy-start.38 = (bf16[1600]{0:T(1024)(128)(2,1)S(1)}, bf16[1600]{0:T(1024)(128)(2,1)}, u32[]{:S(2)}) copy-start(bf16[1600]{0:T(1024)(128)(2,1)} %get-tuple-element.460) | copy-start | bytes 9604
  1283.0 56.7 %copy-start.5 = (f32[128,1600]{0,1:T(8,128)S(1)}, f32[128,1600]{0,1:T(8,128)}, u32[]{:S(2)}) copy-start(f32[128,1600]{0,1:T(8,128)} %copy-done.4) | copy-start | bytes 2457604
  1283.1 56.7 %copy-start.9 = (bf16[128,1600]{0,1:T(8,128)(2,1)S(1)}, bf16[128,1600]{0,1:T(8,128)(2,1)}, u32[]{:S(2)}) copy-start(bf16[128,1600]{0,1:T(8,128)(2,1)} %copy.92) | copy-start | bytes 1228804
  1283.1 56.7 %copy-start.15 = (bf16[128,1600]{0,1:T(8,128)(2,1)S(1)}, bf16[128,1600]{0,1:T(8,128)(2,1)}, u32[]{:S(2)}) copy-start(bf16[128,1600]{0,1:T(8,128)(2,1)} %param.37) | copy-start | bytes 1228804
  1283.1 56.6 %copy-start.32 = (f32[1600]{0:T(1024)S(1)}, f32[1600]{0:T(1024)}, u32[]{:S(2)}) copy-start(f32[1600]{0:T(1024)} %get-tuple-element.378) | copy-start | bytes 19204
  1491.8 7.5 copy-start.13
  (28 other events, 78.5 us)
Sparse Core Ops, SparseCore 0:
  9.6 269.7 all-gather.5
  292.8 31.5 all-gather.9
  326.9 33.2 all-gather.7
  361.6 83.6 all-gather.13
  499.8 52.6 all-gather.11
  577.6 35.5 reduce-scatter.20
  680.4 46.2 reduce-scatter.22
  730.7 47.3 reduce-scatter.24
  781.0 164.4 reduce-scatter.16
  947.7 294.4 reduce-scatter.14
  1245.1 36.4 reduce-scatter.18
  1286.1 205.6 all-reduce.15
